TPU v7x, 32 devices: a whole 2x2x4 slice. The times are simulated.
32 devices in a mesh: groups: 2 (over x), blk: 16 (over z, y, core).
Axes of the slice: x: 2, y: 2, z: 4, core: 2. Of those that a mesh axis runs over, the one named last changes fastest.
Arguments:
- queries: bfloat16 [4096, 4096], P(('groups', 'blk')), parts along dimension 0, may hold values from -96 to 96
- keys: bfloat16 [4096, 512], P(('groups', 'blk')), parts along dimension 0, may hold values from -3 to 3
- values: bfloat16 [4096, 512], P(('groups', 'blk')), parts along dimension 0, may hold values from -4 to 4
- out_packed: int32 [4096, 512], P('blk'), may hold values from -2147483648 to 2147483646
- out_scales: bfloat16 [32, 4096], replicated, may hold values from 0.0029907227 to 0.029907227
- hadamard_signs: int32 [4096], replicated, may hold values from 0 to 1
Outputs:
- mixed: bfloat16 [4096, 4096], P(('groups', 'blk')), parts along dimension 0
There are 2 independent parts, one for each index of `groups`. A program takes and returns all parts, laid end to end along the dimension named above; an argument that names none is the same for every part. Nothing has to cross between parts.
All inputs are finite; a program needn't handle non-finite values.
Results may differ from a plain program's by a relative error of at most 0.012.
Values may be sent and summed in bfloat16 or wider, within the bound.
A program may use at most 256 MiB of HBM per device.

v0:
```python
import math
import jax
import jax.numpy as jnp
from jax import lax
from jax.sharding import PartitionSpec as P

HEAD_SIZE = 128
QUERY_HEADS = 32
KEY_VALUE_HEADS = 4
GROUP = 128
masked_fill_value = -1e30


def sylvester(block_count):
    index = jnp.arange(block_count, dtype=jnp.int32)
    both = jnp.bitwise_and(index[:, None], index[None, :])
    parity = jnp.zeros((block_count, block_count), jnp.int32)
    for bit_number in range(block_count.bit_length() - 1):
        parity = jnp.bitwise_xor(parity, jnp.bitwise_and(jnp.right_shift(both, bit_number), 1))
    return (1 - 2 * parity).astype(jnp.bfloat16)


def rotate(attention, hadamard_signs):
    block_count = attention.shape[0]
    signed = (attention * (2 * hadamard_signs - 1).astype(jnp.bfloat16)).reshape(
        block_count, QUERY_HEADS, HEAD_SIZE
    )
    outer = jnp.einsum(
        "gh,rhd->rgd", sylvester(QUERY_HEADS), signed, preferred_element_type=jnp.float32
    )
    upper = outer.astype(jnp.bfloat16)
    lower = (outer - upper.astype(jnp.float32)).astype(jnp.bfloat16)
    inner_table = sylvester(HEAD_SIZE)
    inner = jnp.einsum("rgd,de->rge", upper, inner_table, preferred_element_type=jnp.float32)
    inner = inner + jnp.einsum(
        "rgd,de->rge", lower, inner_table, preferred_element_type=jnp.float32
    )
    return (
        (inner * (1.0 / math.sqrt(QUERY_HEADS * HEAD_SIZE)))
        .reshape(block_count, QUERY_HEADS * HEAD_SIZE)
        .astype(jnp.bfloat16)
    )


def dequantize_rows(packed, out_scales):
    block_count = packed.shape[0]
    group_count = out_scales.shape[0]
    group_index = jnp.arange(block_count, dtype=jnp.int32) // GROUP
    member = (group_index[:, None] == jnp.arange(group_count, dtype=jnp.int32)[None, :]).astype(
        jnp.bfloat16
    )
    scale_rows = jnp.dot(member, out_scales, preferred_element_type=jnp.float32)
    fields = [jnp.bitwise_and(jnp.right_shift(packed, 4 * nibble), 15) for nibble in range(8)]
    levels = jnp.concatenate(fields, axis=1) - 8
    return (levels.astype(jnp.float32) * scale_rows).astype(jnp.bfloat16)


def update(state, query_tile, query_positions, key_block, value_block, key_positions):
    largest, totals, summed = state
    scores = jnp.einsum("qkgd,nkd->kgqn", query_tile, key_block, preferred_element_type=jnp.float32)
    scores = scores * (1.0 / math.sqrt(HEAD_SIZE))
    allowed = query_positions[:, None] >= key_positions[None, :]
    scores = jnp.where(allowed, scores, masked_fill_value)
    new_largest = jnp.maximum(largest, jnp.max(scores, axis=-1))
    fading = jnp.exp(largest - new_largest)
    weights = jnp.exp(scores - new_largest[..., None])
    totals = totals * fading + jnp.sum(weights, axis=-1)
    product = jnp.einsum(
        "kgqn,nkd->qkgd",
        weights.astype(jnp.bfloat16),
        value_block,
        preferred_element_type=jnp.float32,
    )
    summed = summed * jnp.transpose(fading, (2, 0, 1))[..., None] + product
    return (new_largest, totals, summed)


def keep_state(current):
    return current


def local(queries, keys, values, out_packed, out_scales, hadamard_signs):
    sequence_rows = queries.shape[0]
    my_index = lax.axis_index("blk")
    head_group = QUERY_HEADS // KEY_VALUE_HEADS
    query_positions = my_index * sequence_rows + jnp.arange(sequence_rows, dtype=jnp.int32)
    rows_of_queries = queries.reshape(sequence_rows, KEY_VALUE_HEADS, head_group, HEAD_SIZE)
    initial = (
        jnp.full((KEY_VALUE_HEADS, head_group, sequence_rows), masked_fill_value, jnp.float32),
        jnp.zeros((KEY_VALUE_HEADS, head_group, sequence_rows), jnp.float32),
        jnp.zeros((sequence_rows, KEY_VALUE_HEADS, head_group, HEAD_SIZE), jnp.float32),
    )
    last_position = jnp.max(query_positions)
    key_slice = lax.all_gather(keys, "blk", axis=0, tiled=True)
    value_slice = lax.all_gather(values, "blk", axis=0, tiled=True)
    block_count = key_slice.shape[0]
    width = math.gcd(block_count, 512)
    heads_of_keys = key_slice.reshape(block_count, KEY_VALUE_HEADS, HEAD_SIZE)
    heads_of_values = value_slice.reshape(block_count, KEY_VALUE_HEADS, HEAD_SIZE)

    def sweep(current):

        def one_step(turn, inner_state):
            begin = turn * width
            key_block = lax.dynamic_slice_in_dim(heads_of_keys, begin, width, 0)
            value_block = lax.dynamic_slice_in_dim(heads_of_values, begin, width, 0)
            key_positions = begin + jnp.arange(width, dtype=jnp.int32)
            return update(
                inner_state, rows_of_queries, query_positions, key_block, value_block, key_positions
            )

        return lax.fori_loop(0, block_count // width, one_step, current)

    final = lax.cond(jnp.int32(0) <= last_position, sweep, keep_state, initial)
    largest, totals, summed = final
    attention = (
        (summed / jnp.transpose(totals, (2, 0, 1))[..., None])
        .reshape(sequence_rows, QUERY_HEADS * HEAD_SIZE)
        .astype(jnp.bfloat16)
    )
    rotated = rotate(attention, hadamard_signs)
    weight = dequantize_rows(lax.all_gather(out_packed, "blk", axis=0, tiled=True), out_scales)
    mixed = jnp.dot(rotated, weight, preferred_element_type=jnp.float32)
    return mixed.astype(jnp.bfloat16)


def solution(mesh):
    in_specs = (
        P(("groups", "blk"), None),
        P(("groups", "blk"), None),
        P(("groups", "blk"), None),
        P("blk", None),
        P(),
        P(),
    )
    out_specs = P(("groups", "blk"), None)
    return jax.shard_map(local, mesh=mesh, in_specs=in_specs, out_specs=out_specs, check_vma=False)
```

profile of v0, /device:TPU:0, one launch (start us, length us, event | category | flops | bytes accessed | tf_op | source)
XLA Modules:
  0.0 240.5 jit_solution(12664698832807533376)
XLA Ops:
  12.6 40.6 %all-gather.4.cloned.1.call-done = bf16[2048,512]{0,1:T(8,128)(2,1)} async-done(((bf16[128,512]{0,1:T(8,128)(2,1)}), bf16[2048,512]{0,1:T(8,128)(2,1)}) %all-gather.4.cloned.1.call-update) | async-done | bytes 2097168 | tf_op jit(solution)/shard_map/all_gather | solution.py:94
  53.3 42.3 %all-gather.6.cloned.1.call-done = bf16[2048,512]{0,1:T(8,128)(2,1)} async-done(((bf16[128,512]{0,1:T(8,128)(2,1)}), bf16[2048,512]{0,1:T(8,128)(2,1)}) %all-gather.6.cloned.1.call-update) | async-done | bytes 2097168 | tf_op jit(solution)/shard_map/all_gather | solution.py:95
  95.6 69.5 %conditional.1 = (f32[4,8,128]{2,1,0:T(8,128)}, f32[128,4,8,128]{0,3,2,1:T(8,128)}) conditional(s32[]{:T(128)} %convert_element_type.53, () %tuple.27, (bf16[2048,512]{0,1:T(8,128)(2,1)}, bf16[2048,512]{0,1:T(8,128)(2,1)}, bf16[128,4096]{1,0:T(8,128)(2,1)}, s32[128]{0:T(128)S(1)}) %tuple.28), branch_computations={%region_1.0_spmd, %region_2.7_spmd} | conditional | flops 1098473984 | bytes 69735248 | solution.py:114
  97.9 67.2 %while.17 = (s32[]{:T(128)}, f32[4,8,128]{2,1,0:T(8,128)S(1)}, f32[4,8,128]{2,1,0:T(8,128)}, f32[128,4,8,128]{0,3,2,1:T(8,128)}, s32[128]{0:T(128)S(1)}, /*index...) while((s32[]{:T(128)}, f32[4,8,128]{2,1,0:T(8,128)S(1)}, ...), condition=%wide.region_6.6_spmd.clone, body=%wide.region_3.5_spmd.clone.sunk | while | flops 1098473984 | bytes 65540820 | solution.py:112
  98.1 5.7 %fusion.87 = (f32[4,8,128]{2,1,0:T(8,128)S(1)}, f32[4,512,128,8]{2,1,3,0:T(8,128)}) fusion(pred[128,512]{0,1:T(8,128)(4,1)S(1)} %broadcast_compare_fusion.2, bf16[128,4,8,128]{3,0,2,1:T(8,128)(2,1)S(1)} %get-tuple-element.326, bf16[2048,4,128]{0,2,1:T(8,128)(2,1)} %get-tuple-element.325, s32[]{:T(128)S(6)} %select_n.46), kind=kOutput, calls=%fused_computation.4.clone.1 | convolution fusion | flops 543158272 | bytes 10043396 | tf_op jit(solution)/shard_map/cond/branch_1_fun/while/body/eval_jaxpr/qkgd,nkd->kgqn/dot_general | solution.py:60
  103.8 7.6 %bitcast_add_fusion.2 = f32[128,4,8,128]{0,3,2,1:T(8,128)} fusion(f32[128,4,8,128]{0,3,2,1:T(8,128)} %get-tuple-element.311, f32[4,512,128,8]{2,1,3,0:T(8,128)} %get-tuple-element.294, f32[4,8,128]{2,1,0:T(8,128)S(1)} %get-tuple-element.321, pred[128,512]{0,1:T(8,128)(4,1)S(1)} %broadcast_compare_fusion.2, f32[128,4,8]{0,2,1:T(8,128)S(1)} %get-tuple-element.295, ...), kind=kOutput, calls=%fused_computation.10.clone.1 | convolution fusion | flops 546832384 | bytes 13205509 | tf_op jit(solution)/shard_map/cond/branch_1_fun/while/body/eval_jaxpr/kgqn,nkd->qkgd/dot_general | solution.py:68
  111.4 1.8 fusion.89
  114.0 5.7 %fusion.87 = (f32[4,8,128]{2,1,0:T(8,128)S(1)}, f32[4,512,128,8]{2,1,3,0:T(8,128)}) fusion(pred[128,512]{0,1:T(8,128)(4,1)S(1)} %broadcast_compare_fusion.2, bf16[128,4,8,128]{3,0,2,1:T(8,128)(2,1)S(1)} %get-tuple-element.326, bf16[2048,4,128]{0,2,1:T(8,128)(2,1)} %get-tuple-element.325, s32[]{:T(128)S(6)} %select_n.46), kind=kOutput, calls=%fused_computation.4.clone.1 | convolution fusion | flops 543158272 | bytes 10043396 | tf_op jit(solution)/shard_map/cond/branch_1_fun/while/body/eval_jaxpr/qkgd,nkd->kgqn/dot_general | solution.py:60
  119.8 7.9 %bitcast_add_fusion.2 = f32[128,4,8,128]{0,3,2,1:T(8,128)} fusion(f32[128,4,8,128]{0,3,2,1:T(8,128)} %get-tuple-element.311, f32[4,512,128,8]{2,1,3,0:T(8,128)} %get-tuple-element.294, f32[4,8,128]{2,1,0:T(8,128)S(1)} %get-tuple-element.321, pred[128,512]{0,1:T(8,128)(4,1)S(1)} %broadcast_compare_fusion.2, f32[128,4,8]{0,2,1:T(8,128)S(1)} %get-tuple-element.295, ...), kind=kOutput, calls=%fused_computation.10.clone.1 | convolution fusion | flops 546832384 | bytes 13205509 | tf_op jit(solution)/shard_map/cond/branch_1_fun/while/body/eval_jaxpr/kgqn,nkd->qkgd/dot_general | solution.py:68
  127.6 1.8 fusion.89
  130.9 5.8 %fusion.87 = (f32[4,8,128]{2,1,0:T(8,128)S(1)}, f32[4,512,128,8]{2,1,3,0:T(8,128)}) fusion(pred[128,512]{0,1:T(8,128)(4,1)S(1)} %broadcast_compare_fusion.2, bf16[128,4,8,128]{3,0,2,1:T(8,128)(2,1)S(1)} %get-tuple-element.326, bf16[2048,4,128]{0,2,1:T(8,128)(2,1)} %get-tuple-element.325, s32[]{:T(128)S(6)} %select_n.46), kind=kOutput, calls=%fused_computation.4.clone.1 | convolution fusion | flops 543158272 | bytes 10043396 | tf_op jit(solution)/shard_map/cond/branch_1_fun/while/body/eval_jaxpr/qkgd,nkd->kgqn/dot_general | solution.py:60
  136.7 8.0 %bitcast_add_fusion.2 = f32[128,4,8,128]{0,3,2,1:T(8,128)} fusion(f32[128,4,8,128]{0,3,2,1:T(8,128)} %get-tuple-element.311, f32[4,512,128,8]{2,1,3,0:T(8,128)} %get-tuple-element.294, f32[4,8,128]{2,1,0:T(8,128)S(1)} %get-tuple-element.321, pred[128,512]{0,1:T(8,128)(4,1)S(1)} %broadcast_compare_fusion.2, f32[128,4,8]{0,2,1:T(8,128)S(1)} %get-tuple-element.295, ...), kind=kOutput, calls=%fused_computation.10.clone.1 | convolution fusion | flops 546832384 | bytes 13205509 | tf_op jit(solution)/shard_map/cond/branch_1_fun/while/body/eval_jaxpr/kgqn,nkd->qkgd/dot_general | solution.py:68
  148.0 5.7 %fusion.87 = (f32[4,8,128]{2,1,0:T(8,128)S(1)}, f32[4,512,128,8]{2,1,3,0:T(8,128)}) fusion(pred[128,512]{0,1:T(8,128)(4,1)S(1)} %broadcast_compare_fusion.2, bf16[128,4,8,128]{3,0,2,1:T(8,128)(2,1)S(1)} %get-tuple-element.326, bf16[2048,4,128]{0,2,1:T(8,128)(2,1)} %get-tuple-element.325, s32[]{:T(128)S(6)} %select_n.46), kind=kOutput, calls=%fused_computation.4.clone.1 | convolution fusion | flops 543158272 | bytes 10043396 | tf_op jit(solution)/shard_map/cond/branch_1_fun/while/body/eval_jaxpr/qkgd,nkd->kgqn/dot_general | solution.py:60
  153.7 8.2 %bitcast_add_fusion.2 = f32[128,4,8,128]{0,3,2,1:T(8,128)} fusion(f32[128,4,8,128]{0,3,2,1:T(8,128)} %get-tuple-element.311, f32[4,512,128,8]{2,1,3,0:T(8,128)} %get-tuple-element.294, f32[4,8,128]{2,1,0:T(8,128)S(1)} %get-tuple-element.321, pred[128,512]{0,1:T(8,128)(4,1)S(1)} %broadcast_compare_fusion.2, f32[128,4,8]{0,2,1:T(8,128)S(1)} %get-tuple-element.295, ...), kind=kOutput, calls=%fused_computation.10.clone.1 | convolution fusion | flops 546832384 | bytes 13205509 | tf_op jit(solution)/shard_map/cond/branch_1_fun/while/body/eval_jaxpr/kgqn,nkd->qkgd/dot_general | solution.py:68
  165.1 1.8 divide_convert_fusion
  171.2 7.8 %and_dynamic-update-slice_fusion.7 = s32[4096,4096]{1,0:T(8,128)} fusion(s32[4096,512]{1,0:T(8,128)} %all-gather.8.cloned.1.call-done), kind=kLoop, calls=%fused_computation.37 | loop fusion | flops 4194303 | bytes 16777216
  179.0 4.3 %and_dynamic-update-slice_fusion.6 = s32[4096,4096]{1,0:T(8,128)} fusion(s32[4096,4096]{1,0:T(8,128)} %and_dynamic-update-slice_fusion.7, s32[4096,512]{1,0:T(8,128)S(1)} %copy-done.2), kind=kLoop, calls=%fused_computation.36 | loop fusion | flops 4194304 | bytes 16777216
  183.3 4.3 %and_dynamic-update-slice_fusion.5 = s32[4096,4096]{1,0:T(8,128)} fusion(s32[4096,4096]{1,0:T(8,128)} %and_dynamic-update-slice_fusion.6, s32[4096,512]{1,0:T(8,128)S(1)} %copy-done.2), kind=kLoop, calls=%fused_computation.35 | loop fusion | flops 4194304 | bytes 16777216
  187.5 4.2 %and_dynamic-update-slice_fusion.4 = s32[4096,4096]{1,0:T(8,128)} fusion(s32[4096,4096]{1,0:T(8,128)} %and_dynamic-update-slice_fusion.5, s32[4096,512]{1,0:T(8,128)S(1)} %copy-done.2), kind=kLoop, calls=%fused_computation.34 | loop fusion | flops 4194304 | bytes 16777216
  191.8 4.3 %and_dynamic-update-slice_fusion.3 = s32[4096,4096]{1,0:T(8,128)} fusion(s32[4096,4096]{1,0:T(8,128)} %and_dynamic-update-slice_fusion.4, s32[4096,512]{1,0:T(8,128)S(1)} %copy-done.2), kind=kLoop, calls=%fused_computation.33 | loop fusion | flops 4194304 | bytes 16777216
  196.0 4.2 %and_dynamic-update-slice_fusion.2 = s32[4096,4096]{1,0:T(8,128)} fusion(s32[4096,4096]{1,0:T(8,128)} %and_dynamic-update-slice_fusion.3, s32[4096,512]{1,0:T(8,128)S(1)} %copy-done.2), kind=kLoop, calls=%fused_computation.32 | loop fusion | flops 4194304 | bytes 16777216
  200.3 4.3 %and_dynamic-update-slice_fusion.1 = s32[4096,4096]{1,0:T(8,128)} fusion(s32[4096,4096]{1,0:T(8,128)} %and_dynamic-update-slice_fusion.2, s32[4096,512]{1,0:T(8,128)S(1)} %copy-done.2), kind=kLoop, calls=%fused_computation.31 | loop fusion | flops 4194304 | bytes 16777216
  204.6 4.3 %and_dynamic-update-slice_fusion = s32[4096,4096]{1,0:T(8,128)} fusion(s32[4096,4096]{1,0:T(8,128)} %and_dynamic-update-slice_fusion.1, s32[4096,512]{1,0:T(8,128)S(1)} %copy-done.2), kind=kLoop, calls=%fused_computation.30 | loop fusion | flops 4194304 | bytes 16777216 | tf_op jit(solution)/shard_map/concatenate | solution.py:54
  208.9 25.0 %fusion.23 = bf16[128,4096]{1,0:T(8,128)(2,1)} fusion(bf16[128,4096]{0,1:T(8,128)(2,1)S(1)} %bitcast.70, s32[4096,4096]{1,0:T(8,128)} %and_dynamic-update-slice_fusion, bf16[32,4096]{1,0:T(8,128)(2,1)S(1)} %copy-done, s32[4096]{0:T(1024)S(1)} %add_select_fusion), kind=kOutput, calls=%fused_computation.38 | convolution fusion | flops 5436473344 | bytes 69484544 | tf_op jit(solution)/shard_map/dot_general | solution.py:123
  (56 shorter events, 20.9 us)
Async XLA Ops:
  6.5 202.4 %copy-start = (bf16[32,4096]{1,0:T(8,128)(2,1)S(1)}, bf16[32,4096]{1,0:T(8,128)(2,1)}, u32[]{:S(2)}) copy-start(bf16[32,4096]{1,0:T(8,128)(2,1)} %param.14) | copy-start | bytes 786436
  6.5 46.7 %all-gather.4.cloned.1.call-start = ((), (), s32[]{:S(2)}) async-start(), calls=%async_computation | async-start | bytes 2228224 | tf_op jit(solution)/shard_map/all_gather | solution.py:94
  8.3 87.3 %all-gather.6.cloned.1.call-start = ((), (), s32[]{:S(2)}) async-start(), calls=%async_computation.1 | async-start | bytes 2228224 | tf_op jit(solution)/shard_map/all_gather | solution.py:95
  10.0 161.2 %all-gather.8.cloned.1.call-start = ((), (), s32[]{:S(2)}) async-start(), calls=%async_computation.2 | async-start | bytes 8912896 | tf_op jit(solution)/shard_map/all_gather | solution.py:122
  103.8 7.6 %copy-start.1 = (f32[4,512,128,8]{2,1,3,0:T(8,128)S(1)}, f32[4,512,128,8]{2,1,3,0:T(8,128)}, u32[]{:S(2)}) copy-start(f32[4,512,128,8]{2,1,3,0:T(8,128)} %get-tuple-element.294) | copy-start | bytes 25165828 | tf_op jit(solution)/shard_map/cond/branch_1_fun/while
  119.7 7.9 %copy-start.1 = (f32[4,512,128,8]{2,1,3,0:T(8,128)S(1)}, f32[4,512,128,8]{2,1,3,0:T(8,128)}, u32[]{:S(2)}) copy-start(f32[4,512,128,8]{2,1,3,0:T(8,128)} %get-tuple-element.294) | copy-start | bytes 25165828 | tf_op jit(solution)/shard_map/cond/branch_1_fun/while
  136.7 8.0 %copy-start.1 = (f32[4,512,128,8]{2,1,3,0:T(8,128)S(1)}, f32[4,512,128,8]{2,1,3,0:T(8,128)}, u32[]{:S(2)}) copy-start(f32[4,512,128,8]{2,1,3,0:T(8,128)} %get-tuple-element.294) | copy-start | bytes 25165828 | tf_op jit(solution)/shard_map/cond/branch_1_fun/while
  153.7 8.2 %copy-start.1 = (f32[4,512,128,8]{2,1,3,0:T(8,128)S(1)}, f32[4,512,128,8]{2,1,3,0:T(8,128)}, u32[]{:S(2)}) copy-start(f32[4,512,128,8]{2,1,3,0:T(8,128)} %get-tuple-element.294) | copy-start | bytes 25165828 | tf_op jit(solution)/shard_map/cond/branch_1_fun/while
  171.2 7.8 %copy-start.2 = (s32[4096,512]{1,0:T(8,128)S(1)}, s32[4096,512]{1,0:T(8,128)}, u32[]{:S(2)}) copy-start(s32[4096,512]{1,0:T(8,128)} %all-gather.8.cloned.1.call-done) | copy-start | bytes 25165828
Sparse Core Ops, SparseCore 0:
  9.5 43.7 all-gather.3
  55.4 40.1 all-gather.5
  97.8 73.3 all-gather.7
where the time goes:
time: 241 us; the launch traced here: 240 us
  waiting for transfers between devices  85.2 us (35%)
  matrix products  81.3 us (34%)
  other arithmetic  53.4 us (22%)
  between operations  13.7 us (6%)
  local copies, waits for them, and re-layouts  6.64 us (3%)
    all_gather x1, waiting for transfers between devices, local(): value_slice = lax.all_gather(values, 'blk', axis=0, tiled=True)  42.3 us
    all_gather x1, waiting for transfers between devices, local(): key_slice = lax.all_gather(keys, 'blk', axis=0, tiled=True)  40.6 us
    unnamed x7, other arithmetic  33.4 us
    dot_general x4, matrix products, update(): jnp.einsum('kgqn,nkd->qkgd', weights.astype(jnp.bfloat16), value_block, p...  31.6 us
    dot_general x1, matrix products, local(): mixed = jnp.dot(rotated, weight, preferred_element_type=jnp.float32)  25 us
    dot_general x4, matrix products, update(): jnp.einsum('qkgd,nkd->kgqn', query_tile, key_block, preferred_element_typ...  22.9 us
    reduce_sum x4, other arithmetic, update(): totals = totals * fading + jnp.sum(weights, axis=-1)  7.23 us
  transfers between devices with their start and end apart: 3, of which 3 were waited for; matrix products, arithmetic and copies ran while one was open for 32% of the time, Pallas kernels for 0%

commit v1 on v0

--- a/solution.py
+++ b/solution.py
@@ -9,6 +9,12 @@
 KEY_VALUE_HEADS = 4
 GROUP = 128
 masked_fill_value = -1e30
+
+
+def _hold_rows(xx, axis_tag, work_x):
+    u_next = jnp.concatenate([work_x, xx], 1)
+    found_now = jax.lax.all_gather(u_next, axis_tag, tiled=True, axis=0)
+    return jnp.split(found_now, [work_x.shape[1]], 1)
 
 
 def sylvester(block_count):
@@ -91,8 +97,7 @@
         jnp.zeros((sequence_rows, KEY_VALUE_HEADS, head_group, HEAD_SIZE), jnp.float32),
     )
     last_position = jnp.max(query_positions)
-    key_slice = lax.all_gather(keys, "blk", axis=0, tiled=True)
-    value_slice = lax.all_gather(values, "blk", axis=0, tiled=True)
+    key_slice, value_slice = _hold_rows(values, "blk", keys)
     block_count = key_slice.shape[0]
     width = math.gcd(block_count, 512)
     heads_of_keys = key_slice.reshape(block_count, KEY_VALUE_HEADS, HEAD_SIZE)

time: 241 us -> 210 us (0.87)
  waiting for transfers between devices: 85.2 us -> 53.7 us
  matrix products: 81.3 us -> 76.6 us
  local copies, waits for them, and re-layouts: 6.64 us -> 10.1 us
    all_gather x2 -> x1, waiting for transfers between devices: 82.9 us -> 52.5 us  [_hold_rows(): found_now = jax.lax.all_gather(u_next, axis_tag, tiled=True, axis=0)]
    dot_general x4, matrix products: 22.9 us -> 18.7 us  [update(): jnp.einsum('qkgd,nkd->kgqn', query_tile, key_block, preferred_element_typ...]
    split x0 -> x1, local copies, waits for them, and re-layouts: none -> 4.08 us  [_hold_rows(): return jnp.split(found_now, [work_x.shape[1]], 1)]
  transfers between devices with their start and end apart: 3 -> 2, of which waited for: 3 -> 2; matrix products, arithmetic and copies ran while one was open for 32% -> 36% of each run, Pallas kernels for 0% -> 0%
where the time goes in v1:
time: 210 us; the launch traced here: 209 us
  matrix products  76.6 us (36%)
  other arithmetic  54.3 us (26%)
  waiting for transfers between devices  53.7 us (26%)
  between operations  14.2 us (7%)
  local copies, waits for them, and re-layouts  10.1 us (5%)
    all_gather x1, waiting for transfers between devices, _hold_rows(): found_now = jax.lax.all_gather(u_next, axis_tag, tiled=True, axis=0)  52.5 us
    unnamed x7, other arithmetic  33.4 us
    dot_general x4, matrix products, update(): jnp.einsum('kgqn,nkd->qkgd', weights.astype(jnp.bfloat16), value_block, p...  31.1 us
    dot_general x1, matrix products, local(): mixed = jnp.dot(rotated, weight, preferred_element_type=jnp.float32)  25 us
    dot_general x4, matrix products, update(): jnp.einsum('qkgd,nkd->kgqn', query_tile, key_block, preferred_element_typ...  18.7 us
    reduce_sum x4, other arithmetic, update(): totals = totals * fading + jnp.sum(weights, axis=-1)  7.23 us
    add x4, other arithmetic, update(): totals = totals * fading + jnp.sum(weights, axis=-1)  4.67 us
    concatenate x1, other arithmetic, dequantize_rows(): levels = jnp.concatenate(fields, axis=1) - 8  4.28 us
  transfers between devices with their start and end apart: 2, of which 2 were waited for; matrix products, arithmetic and copies ran while one was open for 36% of the time, Pallas kernels for 0%

profile of v1, /device:TPU:0, one launch (start us, length us, event | category | flops | bytes accessed | tf_op | source)
XLA Modules:
  0.0 209.0 jit_solution(16537927073208589743)
XLA Ops:
  12.3 52.5 %all-gather.3.cloned.1.call-done = bf16[2048,1024]{0,1:T(8,128)(2,1)} async-done(((bf16[128,1024]{0,1:T(8,128)(2,1)}), bf16[2048,1024]{0,1:T(8,128)(2,1)}) %all-gather.3.cloned.1.call-update) | async-done | bytes 4194320 | tf_op jit(solution)/shard_map/all_gather | solution.py:16
  64.8 69.5 %conditional.1 = (f32[4,8,128]{2,1,0:T(8,128)}, f32[128,4,8,128]{0,3,2,1:T(8,128)}) conditional(s32[]{:T(128)} %convert_element_type.53, () %tuple.27, (bf16[2048,1024]{0,1:T(8,128)(2,1)}, bf16[128,4096]{1,0:T(8,128)(2,1)}, s32[128]{0:T(128)S(1)}) %tuple.28), branch_computations={%region_1.0_spmd, %region_2.7_spmd} | conditional | flops 1098473984 | bytes 82318184 | solution.py:119
  64.8 4.1 %fusion.74 = (bf16[2048,512]{0,1:T(8,128)(2,1)}, bf16[2048,512]{0,1:T(8,128)(2,1)S(1)}) fusion(bf16[2048,1024]{0,1:T(8,128)(2,1)} %get-tuple-element.156), kind=kLoop, calls=%fused_computation.99 | loop fusion | bytes 8388608 | tf_op jit(solution)/shard_map/split | solution.py:17
  71.8 62.5 %while.17 = (s32[]{:T(128)}, f32[4,8,128]{2,1,0:T(8,128)S(1)}, f32[4,8,128]{2,1,0:T(8,128)}, f32[128,4,8,128]{0,3,2,1:T(8,128)}, s32[128]{0:T(128)S(1)}, /*index...) while((s32[]{:T(128)}, f32[4,8,128]{2,1,0:T(8,128)S(1)}, ...), condition=%wide.region_6.6_spmd.clone, body=%wide.region_3.5_spmd.clone.sunk | while | flops 1098473984 | bytes 65540820 | solution.py:117
  72.0 4.7 %fusion.88 = (f32[4,8,128]{2,1,0:T(8,128)S(1)}, f32[4,512,128,8]{2,1,3,0:T(8,128)}) fusion(pred[128,512]{0,1:T(8,128)(4,1)S(1)} %broadcast_compare_fusion.2, bf16[128,4,8,128]{3,0,2,1:T(8,128)(2,1)S(1)} %get-tuple-element.326, bf16[2048,4,128]{0,2,1:T(8,128)(2,1)S(1)} %get-tuple-element.325, s32[]{:T(128)S(6)} %select_n.46), kind=kOutput, calls=%fused_computation.4.clone.1 | convolution fusion | flops 543158272 | bytes 10043396 | tf_op jit(solution)/shard_map/cond/branch_1_fun/while/body/eval_jaxpr/qkgd,nkd->kgqn/dot_general | solution.py:66
  76.7 7.2 %bitcast_add_fusion.2 = f32[128,4,8,128]{0,3,2,1:T(8,128)} fusion(f32[128,4,8,128]{0,3,2,1:T(8,128)} %get-tuple-element.311, f32[4,512,128,8]{2,1,3,0:T(8,128)} %get-tuple-element.294, f32[4,8,128]{2,1,0:T(8,128)S(1)} %get-tuple-element.321, pred[128,512]{0,1:T(8,128)(4,1)S(1)} %broadcast_compare_fusion.2, f32[128,4,8]{0,2,1:T(8,128)S(1)} %get-tuple-element.295, ...), kind=kOutput, calls=%fused_computation.10.clone.1 | convolution fusion | flops 546832384 | bytes 13205509 | tf_op jit(solution)/shard_map/cond/branch_1_fun/while/body/eval_jaxpr/kgqn,nkd->qkgd/dot_general | solution.py:74
  83.9 1.8 fusion.90
  86.5 4.7 %fusion.88 = (f32[4,8,128]{2,1,0:T(8,128)S(1)}, f32[4,512,128,8]{2,1,3,0:T(8,128)}) fusion(pred[128,512]{0,1:T(8,128)(4,1)S(1)} %broadcast_compare_fusion.2, bf16[128,4,8,128]{3,0,2,1:T(8,128)(2,1)S(1)} %get-tuple-element.326, bf16[2048,4,128]{0,2,1:T(8,128)(2,1)S(1)} %get-tuple-element.325, s32[]{:T(128)S(6)} %select_n.46), kind=kOutput, calls=%fused_computation.4.clone.1 | convolution fusion | flops 543158272 | bytes 10043396 | tf_op jit(solution)/shard_map/cond/branch_1_fun/while/body/eval_jaxpr/qkgd,nkd->kgqn/dot_general | solution.py:66
  91.2 7.8 %bitcast_add_fusion.2 = f32[128,4,8,128]{0,3,2,1:T(8,128)} fusion(f32[128,4,8,128]{0,3,2,1:T(8,128)} %get-tuple-element.311, f32[4,512,128,8]{2,1,3,0:T(8,128)} %get-tuple-element.294, f32[4,8,128]{2,1,0:T(8,128)S(1)} %get-tuple-element.321, pred[128,512]{0,1:T(8,128)(4,1)S(1)} %broadcast_compare_fusion.2, f32[128,4,8]{0,2,1:T(8,128)S(1)} %get-tuple-element.295, ...), kind=kOutput, calls=%fused_computation.10.clone.1 | convolution fusion | flops 546832384 | bytes 13205509 | tf_op jit(solution)/shard_map/cond/branch_1_fun/while/body/eval_jaxpr/kgqn,nkd->qkgd/dot_general | solution.py:74
  102.3 4.7 %fusion.88 = (f32[4,8,128]{2,1,0:T(8,128)S(1)}, f32[4,512,128,8]{2,1,3,0:T(8,128)}) fusion(pred[128,512]{0,1:T(8,128)(4,1)S(1)} %broadcast_compare_fusion.2, bf16[128,4,8,128]{3,0,2,1:T(8,128)(2,1)S(1)} %get-tuple-element.326, bf16[2048,4,128]{0,2,1:T(8,128)(2,1)S(1)} %get-tuple-element.325, s32[]{:T(128)S(6)} %select_n.46), kind=kOutput, calls=%fused_computation.4.clone.1 | convolution fusion | flops 543158272 | bytes 10043396 | tf_op jit(solution)/shard_map/cond/branch_1_fun/while/body/eval_jaxpr/qkgd,nkd->kgqn/dot_general | solution.py:66
  107.0 7.9 %bitcast_add_fusion.2 = f32[128,4,8,128]{0,3,2,1:T(8,128)} fusion(f32[128,4,8,128]{0,3,2,1:T(8,128)} %get-tuple-element.311, f32[4,512,128,8]{2,1,3,0:T(8,128)} %get-tuple-element.294, f32[4,8,128]{2,1,0:T(8,128)S(1)} %get-tuple-element.321, pred[128,512]{0,1:T(8,128)(4,1)S(1)} %broadcast_compare_fusion.2, f32[128,4,8]{0,2,1:T(8,128)S(1)} %get-tuple-element.295, ...), kind=kOutput, calls=%fused_computation.10.clone.1 | convolution fusion | flops 546832384 | bytes 13205509 | tf_op jit(solution)/shard_map/cond/branch_1_fun/while/body/eval_jaxpr/kgqn,nkd->qkgd/dot_general | solution.py:74
  114.9 1.8 fusion.90
  118.2 4.7 %fusion.88 = (f32[4,8,128]{2,1,0:T(8,128)S(1)}, f32[4,512,128,8]{2,1,3,0:T(8,128)}) fusion(pred[128,512]{0,1:T(8,128)(4,1)S(1)} %broadcast_compare_fusion.2, bf16[128,4,8,128]{3,0,2,1:T(8,128)(2,1)S(1)} %get-tuple-element.326, bf16[2048,4,128]{0,2,1:T(8,128)(2,1)S(1)} %get-tuple-element.325, s32[]{:T(128)S(6)} %select_n.46), kind=kOutput, calls=%fused_computation.4.clone.1 | convolution fusion | flops 543158272 | bytes 10043396 | tf_op jit(solution)/shard_map/cond/branch_1_fun/while/body/eval_jaxpr/qkgd,nkd->kgqn/dot_general | solution.py:66
  122.9 8.2 %bitcast_add_fusion.2 = f32[128,4,8,128]{0,3,2,1:T(8,128)} fusion(f32[128,4,8,128]{0,3,2,1:T(8,128)} %get-tuple-element.311, f32[4,512,128,8]{2,1,3,0:T(8,128)} %get-tuple-element.294, f32[4,8,128]{2,1,0:T(8,128)S(1)} %get-tuple-element.321, pred[128,512]{0,1:T(8,128)(4,1)S(1)} %broadcast_compare_fusion.2, f32[128,4,8]{0,2,1:T(8,128)S(1)} %get-tuple-element.295, ...), kind=kOutput, calls=%fused_computation.10.clone.1 | convolution fusion | flops 546832384 | bytes 13205509 | tf_op jit(solution)/shard_map/cond/branch_1_fun/while/body/eval_jaxpr/kgqn,nkd->qkgd/dot_general | solution.py:74
  134.3 2.0 divide_convert_fusion
  139.4 7.9 %and_dynamic-update-slice_fusion.7 = s32[4096,4096]{1,0:T(8,128)} fusion(s32[4096,512]{1,0:T(8,128)} %all-gather.5.cloned.1.call-done), kind=kLoop, calls=%fused_computation.37 | loop fusion | flops 4194303 | bytes 16777216
  147.3 4.3 %and_dynamic-update-slice_fusion.6 = s32[4096,4096]{1,0:T(8,128)} fusion(s32[4096,4096]{1,0:T(8,128)} %and_dynamic-update-slice_fusion.7, s32[4096,512]{1,0:T(8,128)S(1)} %copy-done.2), kind=kLoop, calls=%fused_computation.36 | loop fusion | flops 4194304 | bytes 16777216
  151.6 4.3 %and_dynamic-update-slice_fusion.5 = s32[4096,4096]{1,0:T(8,128)} fusion(s32[4096,4096]{1,0:T(8,128)} %and_dynamic-update-slice_fusion.6, s32[4096,512]{1,0:T(8,128)S(1)} %copy-done.2), kind=kLoop, calls=%fused_computation.35 | loop fusion | flops 4194304 | bytes 16777216
  155.8 4.3 %and_dynamic-update-slice_fusion.4 = s32[4096,4096]{1,0:T(8,128)} fusion(s32[4096,4096]{1,0:T(8,128)} %and_dynamic-update-slice_fusion.5, s32[4096,512]{1,0:T(8,128)S(1)} %copy-done.2), kind=kLoop, calls=%fused_computation.34 | loop fusion | flops 4194304 | bytes 16777216
  160.1 4.2 %and_dynamic-update-slice_fusion.3 = s32[4096,4096]{1,0:T(8,128)} fusion(s32[4096,4096]{1,0:T(8,128)} %and_dynamic-update-slice_fusion.4, s32[4096,512]{1,0:T(8,128)S(1)} %copy-done.2), kind=kLoop, calls=%fused_computation.33 | loop fusion | flops 4194304 | bytes 16777216
  164.3 4.3 %and_dynamic-update-slice_fusion.2 = s32[4096,4096]{1,0:T(8,128)} fusion(s32[4096,4096]{1,0:T(8,128)} %and_dynamic-update-slice_fusion.3, s32[4096,512]{1,0:T(8,128)S(1)} %copy-done.2), kind=kLoop, calls=%fused_computation.32 | loop fusion | flops 4194304 | bytes 16777216
  168.6 4.2 %and_dynamic-update-slice_fusion.1 = s32[4096,4096]{1,0:T(8,128)} fusion(s32[4096,4096]{1,0:T(8,128)} %and_dynamic-update-slice_fusion.2, s32[4096,512]{1,0:T(8,128)S(1)} %copy-done.2), kind=kLoop, calls=%fused_computation.31 | loop fusion | flops 4194304 | bytes 16777216
  172.8 4.3 %and_dynamic-update-slice_fusion = s32[4096,4096]{1,0:T(8,128)} fusion(s32[4096,4096]{1,0:T(8,128)} %and_dynamic-update-slice_fusion.1, s32[4096,512]{1,0:T(8,128)S(1)} %copy-done.2), kind=kLoop, calls=%fused_computation.30 | loop fusion | flops 4194304 | bytes 16777216 | tf_op jit(solution)/shard_map/concatenate | solution.py:60
  177.1 25.0 %fusion.23 = bf16[128,4096]{1,0:T(8,128)(2,1)} fusion(bf16[128,4096]{0,1:T(8,128)(2,1)S(1)} %bitcast.71, s32[4096,4096]{1,0:T(8,128)} %and_dynamic-update-slice_fusion, bf16[32,4096]{1,0:T(8,128)(2,1)S(1)} %copy-done, s32[4096]{0:T(1024)S(1)} %add_select_fusion), kind=kOutput, calls=%fused_computation.38 | convolution fusion | flops 5436473344 | bytes 69484544 | tf_op jit(solution)/shard_map/dot_general | solution.py:128
  (57 shorter events, 20.0 us)
Async XLA Ops:
  6.5 170.6 %copy-start = (bf16[32,4096]{1,0:T(8,128)(2,1)S(1)}, bf16[32,4096]{1,0:T(8,128)(2,1)}, u32[]{:S(2)}) copy-start(bf16[32,4096]{1,0:T(8,128)(2,1)} %param.14) | copy-start | bytes 786436
  6.5 58.2 %all-gather.3.cloned.1.call-start = ((), (), s32[]{:S(2)}) async-start(), calls=%async_computation | async-start | bytes 4456448 | tf_op jit(solution)/shard_map/all_gather | solution.py:16
  9.4 130.0 %all-gather.5.cloned.1.call-start = ((), (), s32[]{:S(2)}) async-start(), calls=%async_computation.1 | async-start | bytes 8912896 | tf_op jit(solution)/shard_map/all_gather | solution.py:127
  64.8 4.1 %copy-start.3 = (bf16[128,4096]{1,0:T(8,128)(2,1)S(1)}, bf16[128,4096]{1,0:T(8,128)(2,1)}, u32[]{:S(2)}) copy-start(bf16[128,4096]{1,0:T(8,128)(2,1)} %get-tuple-element.213) | copy-start | bytes 3145732 | tf_op jit(solution)/shard_map/cond
  76.6 7.3 %copy-start.1 = (f32[4,512,128,8]{2,1,3,0:T(8,128)S(1)}, f32[4,512,128,8]{2,1,3,0:T(8,128)}, u32[]{:S(2)}) copy-start(f32[4,512,128,8]{2,1,3,0:T(8,128)} %get-tuple-element.294) | copy-start | bytes 25165828 | tf_op jit(solution)/shard_map/cond/branch_1_fun/while
  91.2 7.8 %copy-start.1 = (f32[4,512,128,8]{2,1,3,0:T(8,128)S(1)}, f32[4,512,128,8]{2,1,3,0:T(8,128)}, u32[]{:S(2)}) copy-start(f32[4,512,128,8]{2,1,3,0:T(8,128)} %get-tuple-element.294) | copy-start | bytes 25165828 | tf_op jit(solution)/shard_map/cond/branch_1_fun/while
  107.0 7.9 %copy-start.1 = (f32[4,512,128,8]{2,1,3,0:T(8,128)S(1)}, f32[4,512,128,8]{2,1,3,0:T(8,128)}, u32[]{:S(2)}) copy-start(f32[4,512,128,8]{2,1,3,0:T(8,128)} %get-tuple-element.294) | copy-start | bytes 25165828 | tf_op jit(solution)/shard_map/cond/branch_1_fun/while
  122.9 8.2 %copy-start.1 = (f32[4,512,128,8]{2,1,3,0:T(8,128)S(1)}, f32[4,512,128,8]{2,1,3,0:T(8,128)}, u32[]{:S(2)}) copy-start(f32[4,512,128,8]{2,1,3,0:T(8,128)} %get-tuple-element.294) | copy-start | bytes 25165828 | tf_op jit(solution)/shard_map/cond/branch_1_fun/while
  139.4 7.9 %copy-start.2 = (s32[4096,512]{1,0:T(8,128)S(1)}, s32[4096,512]{1,0:T(8,128)}, u32[]{:S(2)}) copy-start(s32[4096,512]{1,0:T(8,128)} %all-gather.5.cloned.1.call-done) | copy-start | bytes 25165828
Sparse Core Ops, SparseCore 0:
  9.5 55.1 all-gather.2
  66.9 72.4 all-gather.4
